TPU v7x, 32 devices: a whole 2x2x4 slice. The times are simulated.
32 devices in a mesh: row: 8 (over y, x, core), col: 4 (over z).
Axes of the slice: x: 2, y: 2, z: 4, core: 2. Of those that a mesh axis runs over, the one named last changes fastest.
Arguments:
- vectors: float32 [32768, 4096], P('row', 'col'), may hold values from -6 to 6
- reflectors: float32 [8, 32768, 128], P('col', 'row'), may hold values from -0.03125 to 0.03125
- triangles: float32 [8, 128, 128], P('col'), may hold values from -0.25 to 1.8, as said below
Outputs:
- transformed: float32 [32768, 4096], P('row', 'col')
Inputs may be any that keep to these rules, and one draw needn't show every extreme that they name: Each triangles[p] is upper triangular with diagonal entries between 0.5 and 1.8.
All inputs are finite; a program needn't handle non-finite values.
Results may differ from a plain program's by a relative error of at most 0.00013.
Values sent between devices are 32-bit elements; how exact they have to be, the bound alone decides.
A program may use at most 128 MiB of HBM per device.

v0:
```python
import jax
import jax.numpy as jnp
from jax import lax
from jax.sharding import PartitionSpec as P


def spread(block, axis, owner):
    block = jnp.where(lax.axis_index(axis) == owner, block, jnp.zeros_like(block))
    return lax.psum(block, axis)


def product_t(left, right):
    return lax.dot_general(
        left,
        right,
        (((0,), (0,)), ((), ())),
        precision=lax.Precision.HIGHEST,
        preferred_element_type=jnp.float32,
    )


def matmul(left, right):
    return jnp.dot(left, right, precision=lax.Precision.HIGHEST, preferred_element_type=jnp.float32)


def shards(vectors, reflectors, triangles):
    per_dev = reflectors.shape[0]
    panels = per_dev * lax.axis_size("col")

    def fetch(panel):
        local = panel % per_dev
        return (
            spread(reflectors[local], "col", panel // per_dev),
            spread(triangles[local], "col", panel // per_dev),
        )

    block = vectors
    for pair in range(panels // 2 - 1, -1, -1):
        basis_a, tri_a = fetch(2 * pair)
        basis_b, tri_b = fetch(2 * pair + 1)
        joined = jnp.concatenate([basis_a, basis_b], axis=1)
        summed, inner = lax.psum((product_t(joined, block), product_t(basis_a, basis_b)), "row")
        width = basis_a.shape[1]
        upper_w = summed[:width]
        lower_w = summed[width:]
        coupling = -matmul(matmul(tri_a, inner), tri_b)
        scaled_a = matmul(tri_a, upper_w) + matmul(coupling, lower_w)
        scaled_b = matmul(tri_b, lower_w)
        block = block - matmul(joined, jnp.concatenate([scaled_a, scaled_b], axis=0))
    return block


def solution(mesh):
    placed = (P("row", "col"), P("col", "row", None), P("col", None, None))
    return jax.shard_map(
        shards, mesh=mesh, in_specs=placed, out_specs=P("row", "col"), check_vma=False
    )
```

profile of v0, /device:TPU:0, one launch (start us, length us, event | category | flops | bytes accessed | tf_op | source)
XLA Modules:
  0.0 1032.6 jit_solution(5668326063415492051)
XLA Ops:
  6.5 0.0 all-reduce.19.cloned.1.call-start
  6.5 1.7 select_bitcast_fusion.9
  8.2 8.2 select_bitcast_fusion
  16.4 0.0 all-reduce.19.cloned.1.call-update
  16.4 0.0 all-reduce.17.cloned.1.call-start
  16.5 582.0 %all-reduce.19.cloned.1.call-done = (f32[4096,128]{1,0:T(8,128)}, f32[4096,128]{1,0:T(8,128)}, f32[128,128]{1,0:T(8,128)}, f32[128,128]{1,0:T(8,128)}, f32[4096,...) async-done(((f32[4096,128]{1,0:T(8,128)}, ...) | async-done | bytes 17301520 | tf_op jit(solution)/shard_map/psum | solution.py:9
  598.5 1.9 constant_dynamic-update-slice_fusion.1
  600.4 0.3 copy-done.8
  600.7 0.6 copy-done.9
  601.3 4.2 fusion.37
  605.6 0.0 copy-done.3
  605.6 1.5 constant_dynamic-update-slice_fusion.7
  607.1 1.5 constant_dynamic-update-slice_fusion.5
  608.6 1.5 constant_dynamic-update-slice_fusion.3
  610.2 0.2 constant_dynamic-update-slice_fusion
  610.3 0.0 copy-start
  610.3 2.0 copy-done
  612.4 30.1 %fusion.36 = f32[256,1024]{1,0:T(8,128)} fusion(f32[4096,256]{1,0:T(8,128)S(1)} %constant_dynamic-update-slice_fusion, f32[4096,1024]{1,0:T(8,128)} %param.3), kind=kOutput, calls=%fused_computation.72 | convolution fusion | flops 12884901888 | bytes 22020096 | tf_op jit(solution)/shard_map/dot_general | solution.py:13
  642.5 0.0 all-reduce.17.cloned.1.call-update
  642.5 0.3 all-reduce.15.cloned.1.call-start
  642.8 5.7 fusion.40
  648.5 1.5 constant_dynamic-update-slice_fusion.2
  650.0 48.5 %all-reduce.17.cloned.1.call-done = (f32[256,1024]{1,0:T(8,128)}, f32[128,128]{1,0:T(8,128)}) async-done(((f32[256,1024]{1,0:T(8,128)}, f32[128,128]{1,0:T(8,128)}), (f32[256,1024]{1,0:T(8,128)}, f32[128,128]{1,0:T(8,128)})) %all-reduce.17.cloned.1.call-update) | async-done | bytes 1114128 | tf_op jit(solution)/shard_map/psum | solution.py:42
  698.5 0.0 copy-done.17
  698.5 1.2 fusion.38
  699.7 1.7 fusion.18
  701.5 1.6 fusion.29
  703.1 0.2 convolution_negate_fusion.3
  703.3 1.6 convolution_add_fusion.3
  704.9 18.7 %convolution_subtract_fusion.3 = f32[4096,1024]{1,0:T(8,128)} fusion(f32[4096,1024]{1,0:T(8,128)} %param.3, f32[4096,256]{1,0:T(8,128)S(1)} %copy-done.1, f32[128,1024]{1,0:T(8,128)S(1)} %fusion.29, f32[128,1024]{1,0:T(8,128)S(1)} %convolution_add_fusion.3), kind=kOutput, calls=%fused_computation.3 | convolution fusion | flops 12889358336 | bytes 38797312 | tf_op jit(solution)/shard_map/dot_general | solution.py:23
  723.7 18.1 %fusion.39 = f32[256,1024]{1,0:T(8,128)} fusion(f32[4096,256]{1,0:T(8,128)} %constant_dynamic-update-slice_fusion.2, f32[4096,1024]{1,0:T(8,128)} %convolution_subtract_fusion.3), kind=kOutput, calls=%fused_computation.75 | convolution fusion | flops 12884901888 | bytes 22020096 | tf_op jit(solution)/shard_map/dot_general | solution.py:13
  741.8 0.0 all-reduce.15.cloned.1.call-update
  741.8 0.5 all-reduce.13.cloned.1.call-start
  742.4 5.7 fusion.43
  748.1 1.5 constant_dynamic-update-slice_fusion.4
  749.6 48.8 %all-reduce.15.cloned.1.call-done = (f32[256,1024]{1,0:T(8,128)}, f32[128,128]{1,0:T(8,128)}) async-done(((f32[256,1024]{1,0:T(8,128)}, f32[128,128]{1,0:T(8,128)}), (f32[256,1024]{1,0:T(8,128)}, f32[128,128]{1,0:T(8,128)})) %all-reduce.15.cloned.1.call-update) | async-done | bytes 1114128 | tf_op jit(solution)/shard_map/psum | solution.py:42
  798.4 1.0 fusion.41
  799.4 1.6 fusion.16
  801.0 1.6 fusion.26
  802.7 0.2 convolution_negate_fusion.2
  802.9 1.6 convolution_add_fusion.2
  804.5 19.8 %convolution_subtract_fusion.2 = f32[4096,1024]{1,0:T(8,128)} fusion(f32[4096,1024]{1,0:T(8,128)} %convolution_subtract_fusion.3, f32[4096,256]{1,0:T(8,128)} %constant_dynamic-update-slice_fusion.2, f32[128,1024]{1,0:T(8,128)S(1)} %fusion.26, f32[128,1024]{1,0:T(8,128)S(1)} %convolution_add_fusion.2), kind=kOutput, calls=%fused_computation.2 | convolution fusion | flops 12889358336 | bytes 38797312 | tf_op jit(solution)/shard_map/dot_general | solution.py:23
  824.3 18.2 %fusion.42 = f32[256,1024]{1,0:T(8,128)} fusion(f32[4096,256]{1,0:T(8,128)} %constant_dynamic-update-slice_fusion.4, f32[4096,1024]{1,0:T(8,128)} %convolution_subtract_fusion.2), kind=kOutput, calls=%fused_computation.78 | convolution fusion | flops 12884901888 | bytes 22020096 | tf_op jit(solution)/shard_map/dot_general | solution.py:13
  842.4 0.0 all-reduce.13.cloned.1.call-update
  842.5 0.3 all-reduce.11.cloned.1.call-start
  842.7 5.7 fusion.46
  848.4 1.5 constant_dynamic-update-slice_fusion.6
  850.0 49.0 %all-reduce.13.cloned.1.call-done = (f32[256,1024]{1,0:T(8,128)}, f32[128,128]{1,0:T(8,128)}) async-done(((f32[256,1024]{1,0:T(8,128)}, f32[128,128]{1,0:T(8,128)}), (f32[256,1024]{1,0:T(8,128)}, f32[128,128]{1,0:T(8,128)})) %all-reduce.13.cloned.1.call-update) | async-done | bytes 1114128 | tf_op jit(solution)/shard_map/psum | solution.py:42
  899.0 1.0 fusion.44
  900.0 1.6 fusion.14
  901.7 0.0 copy-done.12
  901.7 1.6 fusion.23
  903.3 0.2 convolution_negate_fusion.1
  903.5 1.6 convolution_add_fusion.1
  905.1 19.8 %convolution_subtract_fusion.1 = f32[4096,1024]{1,0:T(8,128)} fusion(f32[4096,1024]{1,0:T(8,128)} %convolution_subtract_fusion.2, f32[4096,256]{1,0:T(8,128)} %constant_dynamic-update-slice_fusion.4, f32[128,1024]{1,0:T(8,128)S(1)} %fusion.23, f32[128,1024]{1,0:T(8,128)S(1)} %convolution_add_fusion.1), kind=kOutput, calls=%fused_computation.1 | convolution fusion | flops 12889358336 | bytes 38797312 | tf_op jit(solution)/shard_map/dot_general | solution.py:23
  925.0 18.0 %fusion.45 = f32[256,1024]{1,0:T(8,128)} fusion(f32[4096,256]{1,0:T(8,128)} %constant_dynamic-update-slice_fusion.6, f32[4096,1024]{1,0:T(8,128)} %convolution_subtract_fusion.1), kind=kOutput, calls=%fused_computation.81 | convolution fusion | flops 12884901888 | bytes 22020096 | tf_op jit(solution)/shard_map/dot_general | solution.py:13
  943.0 0.0 all-reduce.11.cloned.1.call-update
  943.0 56.5 %all-reduce.11.cloned.1.call-done = (f32[256,1024]{1,0:T(8,128)}, f32[128,128]{1,0:T(8,128)}) async-done(((f32[256,1024]{1,0:T(8,128)}, f32[128,128]{1,0:T(8,128)}), (f32[256,1024]{1,0:T(8,128)}, f32[128,128]{1,0:T(8,128)})) %all-reduce.11.cloned.1.call-update) | async-done | bytes 1114128 | tf_op jit(solution)/shard_map/psum | solution.py:42
  999.6 1.0 fusion.47
  1000.6 1.6 fusion.12
  1002.3 1.6 fusion.20
  1003.9 0.2 convolution_negate_fusion
  1004.1 1.6 convolution_add_fusion
  1005.7 19.9 %convolution_subtract_fusion = f32[4096,1024]{1,0:T(8,128)} fusion(f32[4096,1024]{1,0:T(8,128)} %convolution_subtract_fusion.1, f32[4096,256]{1,0:T(8,128)} %constant_dynamic-update-slice_fusion.6, f32[128,1024]{1,0:T(8,128)S(1)} %fusion.20, f32[128,1024]{1,0:T(8,128)S(1)} %convolution_add_fusion), kind=kOutput, calls=%fused_computation | convolution fusion | flops 12889358336 | bytes 38797312 | tf_op jit(solution)/shard_map/dot_general | solution.py:23
  (29 shorter events, 0.1 us)
Async XLA Ops:
  6.5 591.9 %all-reduce.19.cloned.1.call-start = ((), (), s32[]{:S(2)}) async-start(), calls=%async_computation.4 | async-start | bytes 34603008 | tf_op jit(solution)/shard_map/psum | solution.py:9
  16.4 682.1 %all-reduce.17.cloned.1.call-start = ((), (), s32[]{:S(2)}) async-start(), calls=%async_computation.3 | async-start | bytes 2228224 | tf_op jit(solution)/shard_map/psum | solution.py:42
  598.5 2.2 copy-start.8
  598.5 2.9 copy-start.9
  598.5 7.1 copy-start.3
  601.3 5.8 copy-start.5
  605.6 3.1 copy-start.7
  610.3 2.0 copy-start
  612.4 30.4 %copy-start.6 = (f32[4096,128]{1,0:T(8,128)S(1)}, f32[4096,128]{1,0:T(8,128)}, u32[]{:S(2)}) copy-start(f32[4096,128]{1,0:T(8,128)} %get-tuple-element.18) | copy-start | bytes 6291460
  642.5 155.8 %all-reduce.15.cloned.1.call-start = ((), (), s32[]{:S(2)}) async-start(), calls=%async_computation.2 | async-start | bytes 2228224 | tf_op jit(solution)/shard_map/psum | solution.py:42
  642.8 55.7 %copy-start.17 = (f32[128,128]{1,0:T(8,128)S(1)}, f32[128,128]{1,0:T(8,128)}, u32[]{:S(2)}) copy-start(f32[128,128]{1,0:T(8,128)} %get-tuple-element.16) | copy-start | bytes 196612
  642.8 58.6 %copy-start.16 = (f32[128,128]{1,0:T(8,128)S(1)}, f32[128,128]{1,0:T(8,128)}, u32[]{:S(2)}) copy-start(f32[128,128]{1,0:T(8,128)} %get-tuple-element.15) | copy-start | bytes 196612
  698.5 6.4 copy-start.1
  723.7 18.7 %copy-start.4 = (f32[4096,128]{1,0:T(8,128)S(1)}, f32[4096,128]{1,0:T(8,128)}, u32[]{:S(2)}) copy-start(f32[4096,128]{1,0:T(8,128)} %get-tuple-element.22) | copy-start | bytes 6291460
  741.8 157.1 %all-reduce.13.cloned.1.call-start = ((), (), s32[]{:S(2)}) async-start(), calls=%async_computation.1 | async-start | bytes 2228224 | tf_op jit(solution)/shard_map/psum | solution.py:42
  742.4 56.0 %copy-start.15 = (f32[128,128]{1,0:T(8,128)S(1)}, f32[128,128]{1,0:T(8,128)}, u32[]{:S(2)}) copy-start(f32[128,128]{1,0:T(8,128)} %get-tuple-element.20) | copy-start | bytes 196612
  742.4 58.7 %copy-start.14 = (f32[128,128]{1,0:T(8,128)S(1)}, f32[128,128]{1,0:T(8,128)}, u32[]{:S(2)}) copy-start(f32[128,128]{1,0:T(8,128)} %get-tuple-element.19) | copy-start | bytes 196612
  824.3 18.4 %copy-start.2 = (f32[4096,128]{1,0:T(8,128)S(1)}, f32[4096,128]{1,0:T(8,128)}, u32[]{:S(2)}) copy-start(f32[4096,128]{1,0:T(8,128)} %get-tuple-element.26) | copy-start | bytes 6291460
  842.5 157.1 %all-reduce.11.cloned.1.call-start = ((), (), s32[]{:S(2)}) async-start(), calls=%async_computation | async-start | bytes 2228224 | tf_op jit(solution)/shard_map/psum | solution.py:42
  842.7 56.3 %copy-start.13 = (f32[128,128]{1,0:T(8,128)S(1)}, f32[128,128]{1,0:T(8,128)}, u32[]{:S(2)}) copy-start(f32[128,128]{1,0:T(8,128)} %get-tuple-element.24) | copy-start | bytes 196612
  842.7 58.9 %copy-start.12 = (f32[128,128]{1,0:T(8,128)S(1)}, f32[128,128]{1,0:T(8,128)}, u32[]{:S(2)}) copy-start(f32[128,128]{1,0:T(8,128)} %get-tuple-element.23) | copy-start | bytes 196612
  925.0 74.6 %copy-start.11 = (f32[128,128]{1,0:T(8,128)S(1)}, f32[128,128]{1,0:T(8,128)}, u32[]{:S(2)}) copy-start(f32[128,128]{1,0:T(8,128)} %get-tuple-element.28) | copy-start | bytes 196612
  925.0 77.3 %copy-start.10 = (f32[128,128]{1,0:T(8,128)S(1)}, f32[128,128]{1,0:T(8,128)}, u32[]{:S(2)}) copy-start(f32[128,128]{1,0:T(8,128)} %get-tuple-element.27) | copy-start | bytes 196612
Sparse Core Ops, SparseCore 0:
  16.6 581.8 all-reduce.18
  642.6 55.8 all-reduce.16
  742.0 56.3 all-reduce.14
  842.6 56.3 all-reduce.12
  943.2 56.3 all-reduce.10
where the time goes:
time: 1040 us; the launch traced here: 1030 us
  waiting for transfers between devices  785 us (75%)
  matrix products  209 us (20%)
  local copies, waits for them, and re-layouts  14.2 us (1%)
  between operations  14 us (1%)
    psum x1, waiting for transfers between devices, spread(): return lax.psum(block, axis)  582 us
    psum x4, waiting for transfers between devices, shards(): lax.psum((product_t(joined, block), product_t(basis_a, basis_b)), 'row')  203 us
    dot_general x8, matrix products, product_t(): lax.dot_general(left, right, (((0,), (0,)), ((), ())), precision=lax.Prec...  106 us
    dot_general x24, matrix products, matmul(): jnp.dot(left, right, precision=lax.Precision.HIGHEST, preferred_element_t...  103 us
  transfers between devices with their start and end apart: 5, of which 5 were waited for; matrix products, arithmetic and copies ran while one was open for 2% of the time, Pallas kernels for 0%

commit v1 on v0

--- a/solution.py
+++ b/solution.py
@@ -6,7 +6,7 @@
 
 def spread(block, axis, owner):
     block = jnp.where(lax.axis_index(axis) == owner, block, jnp.zeros_like(block))
-    return lax.psum(block, axis)
+    return jnp.sum(lax.all_gather(block, axis), axis=0)
 
 
 def product_t(left, right):

time: 1040 us -> 1570 us (1.51)
  waiting for transfers between devices: 785 us -> 1100 us
  blocking collectives: 0 us -> 149 us
  other arithmetic: 9.88 us -> 47.6 us
  matrix products: 209 us -> 243 us
    all_gather x0 -> x8, waiting for transfers between devices: none -> 929 us  [spread(): return jnp.sum(lax.all_gather(block, axis), axis=0)]
    psum x1 -> x0, waiting for transfers between devices: 582 us -> none  [spread(): return lax.psum(block, axis)]
    all_gather x0 -> x8, blocking collectives: none -> 149 us  [spread(): return jnp.sum(lax.all_gather(block, axis), axis=0)]
    reduce_sum x0 -> x16, other arithmetic: none -> 39.3 us  [spread(): return jnp.sum(lax.all_gather(block, axis), axis=0)]
    dot_general x8, matrix products: 106 us -> 144 us  [product_t(): lax.dot_general(left, right, (((0,), (0,)), ((), ())), precision=lax.Prec...]
    psum x4, waiting for transfers between devices: 203 us -> 170 us  [shards(): lax.psum((product_t(joined, block), product_t(basis_a, basis_b)), 'row')]
  transfers between devices with their start and end apart: 5 -> 12, of which waited for: 5 -> 12; matrix products, arithmetic and copies ran while one was open for 2% -> 13% of each run, Pallas kernels for 0% -> 0%
where the time goes in v1:
time: 1570 us; the launch traced here: 1560 us
  waiting for transfers between devices  1100 us (70%)
  matrix products  243 us (15%)
  blocking collectives  149 us (9%)
  other arithmetic  47.6 us (3%)
    all_gather x8, waiting for transfers between devices, spread(): return jnp.sum(lax.all_gather(block, axis), axis=0)  929 us
    psum x4, waiting for transfers between devices, shards(): lax.psum((product_t(joined, block), product_t(basis_a, basis_b)), 'row')  170 us
    all_gather x8, blocking collectives, spread(): return jnp.sum(lax.all_gather(block, axis), axis=0)  149 us
    dot_general x8, matrix products, product_t(): lax.dot_general(left, right, (((0,), (0,)), ((), ())), precision=lax.Prec...  144 us
    dot_general x24, matrix products, matmul(): jnp.dot(left, right, precision=lax.Precision.HIGHEST, preferred_element_t...  99 us
    reduce_sum x16, other arithmetic, spread(): return jnp.sum(lax.all_gather(block, axis), axis=0)  39.3 us
  transfers between devices with their start and end apart: 12, of which 12 were waited for; matrix products, arithmetic and copies ran while one was open for 13% of the time, Pallas kernels for 0%

profile of v1, /device:TPU:0, one launch (start us, length us, event | category | flops | bytes accessed | tf_op | source)
XLA Modules:
  0.0 1557.9 jit_solution(8890528235720694656)
XLA Ops:
  6.5 8.2 slice_select_fusion.4
  14.8 0.7 all-gather.9.cloned.1.call-update
  15.6 0.7 all-gather.13.cloned.1.call-update
  16.3 0.5 all-gather.15.cloned.1.call-update
  16.9 150.4 %all-gather.11.cloned.1.call-done = f32[4,4096,128]{2,1,0:T(8,128)} async-done(((f32[1,4096,128]{2,1,0:T(8,128)}), f32[4,4096,128]{2,1,0:T(8,128)}) %all-gather.11.cloned.1.call-update) | async-done | bytes 8388624 | tf_op jit(solution)/shard_map/all_gather | solution.py:9
  167.3 4.1 reduce_sum.145
  171.4 145.3 %all-gather.9.cloned.1.call-done = f32[4,4096,128]{2,1,0:T(8,128)} async-done(((f32[1,4096,128]{2,1,0:T(8,128)}), f32[4,4096,128]{2,1,0:T(8,128)}) %all-gather.9.cloned.1.call-update) | async-done | bytes 8388624 | tf_op jit(solution)/shard_map/all_gather | solution.py:9
  316.7 5.4 reduce_sum.144
  322.1 6.1 fusion.44
  328.2 30.4 %fusion.3 = f32[256,1024]{1,0:T(8,128)} fusion(f32[4096,1024]{1,0:T(8,128)} %param.3, f32[4096,128]{1,0:T(8,128)S(1)} %reduce_sum.145, f32[4096,128]{1,0:T(8,128)S(1)} %copy-done.4), kind=kOutput, calls=%fused_computation.11 | convolution fusion | flops 12885950464 | bytes 22020096 | tf_op jit(solution)/shard_map/dot_general | solution.py:13
  358.6 0.5 all-gather.17.cloned.1.call-update
  359.2 0.7 all-gather.19.cloned.1.call-update
  360.4 21.6 %all_gather.67 = f32[4,128,128]{2,1,0:T(8,128)S(1)} all-gather(f32[1,128,128]{2,1,0:T(8,128)S(1)} %get-tuple-element.27), channel_id=1, replica_groups=mesh['row'=8,'col'=4] {'col'}, dimensions={0}, use_global_device_ids=true | all-gather | bytes 327680 | tf_op jit(solution)/shard_map/all_gather | solution.py:9
  382.0 19.6 %all_gather.66 = f32[4,128,128]{2,1,0:T(8,128)S(1)} all-gather(f32[1,128,128]{2,1,0:T(8,128)S(1)} %get-tuple-element.28), channel_id=1, replica_groups=mesh['row'=8,'col'=4] {'col'}, dimensions={0}, use_global_device_ids=true | all-gather | bytes 327680 | tf_op jit(solution)/shard_map/all_gather | solution.py:9
  401.7 72.7 %all-gather.13.cloned.1.call-done = f32[4,4096,128]{2,1,0:T(8,128)} async-done(((f32[1,4096,128]{2,1,0:T(8,128)}), f32[4,4096,128]{2,1,0:T(8,128)}) %all-gather.13.cloned.1.call-update) | async-done | bytes 8388624 | tf_op jit(solution)/shard_map/all_gather | solution.py:9
  474.4 4.1 reduce_sum.148
  478.5 145.2 %all-gather.15.cloned.1.call-done = f32[4,4096,128]{2,1,0:T(8,128)} async-done(((f32[1,4096,128]{2,1,0:T(8,128)}), f32[4,4096,128]{2,1,0:T(8,128)}) %all-gather.15.cloned.1.call-update) | async-done | bytes 8388624 | tf_op jit(solution)/shard_map/all_gather | solution.py:9
  623.7 5.4 reduce_sum.149
  629.1 5.8 fusion.46
  634.9 47.2 %all-reduce.15.cloned.1.call-done = (f32[256,1024]{1,0:T(8,128)}, f32[128,128]{1,0:T(8,128)}) async-done(((f32[256,1024]{1,0:T(8,128)}, f32[128,128]{1,0:T(8,128)}), (f32[256,1024]{1,0:T(8,128)}, f32[128,128]{1,0:T(8,128)})) %all-reduce.15.cloned.1.call-update) | async-done | bytes 1114128 | tf_op jit(solution)/shard_map/psum | solution.py:42
  682.1 1.2 fusion.45
  683.5 1.6 fusion.33
  685.1 1.6 fusion.22
  686.8 1.6 convolution_add_fusion.3
  688.4 19.4 %convolution_subtract_fusion.3 = f32[4096,1024]{1,0:T(8,128)} fusion(f32[4096,1024]{1,0:T(8,128)} %param.3, f32[4096,128]{1,0:T(8,128)S(1)} %copy-done.3, f32[4096,128]{1,0:T(8,128)S(1)} %copy-done.5, f32[128,1024]{1,0:T(8,128)S(1)} %fusion.33, f32[128,1024]{1,0:T(8,128)S(1)} %convolution_add_fusion.3), kind=kOutput, calls=%fused_computation.3 | convolution fusion | flops 12890406912 | bytes 38797312 | tf_op jit(solution)/shard_map/dot_general | solution.py:23
  707.8 30.0 %fusion.2 = f32[256,1024]{1,0:T(8,128)} fusion(f32[4096,1024]{1,0:T(8,128)} %convolution_subtract_fusion.3, f32[4096,128]{1,0:T(8,128)S(1)} %copy-done, f32[4096,128]{1,0:T(8,128)S(1)} %reduce_sum.148), kind=kOutput, calls=%fused_computation.10 | convolution fusion | flops 12885950464 | bytes 22020096 | tf_op jit(solution)/shard_map/dot_general | solution.py:13
  737.9 0.7 all-gather.21.cloned.1.call-update
  738.7 0.5 all-gather.23.cloned.1.call-update
  739.3 19.6 %all_gather.70 = f32[4,128,128]{2,1,0:T(8,128)S(1)} all-gather(f32[1,128,128]{2,1,0:T(8,128)S(1)} %get-tuple-element.22), channel_id=1, replica_groups=mesh['row'=8,'col'=4] {'col'}, dimensions={0}, use_global_device_ids=true | all-gather | bytes 327680 | tf_op jit(solution)/shard_map/all_gather | solution.py:9
  758.9 19.1 %all_gather.71 = f32[4,128,128]{2,1,0:T(8,128)S(1)} all-gather(f32[1,128,128]{2,1,0:T(8,128)S(1)} %get-tuple-element.24), channel_id=1, replica_groups=mesh['row'=8,'col'=4] {'col'}, dimensions={0}, use_global_device_ids=true | all-gather | bytes 327680 | tf_op jit(solution)/shard_map/all_gather | solution.py:9
  778.0 62.7 %all-gather.17.cloned.1.call-done = f32[4,4096,128]{2,1,0:T(8,128)} async-done(((f32[1,4096,128]{2,1,0:T(8,128)}), f32[4,4096,128]{2,1,0:T(8,128)}) %all-gather.17.cloned.1.call-update) | async-done | bytes 8388624 | tf_op jit(solution)/shard_map/all_gather | solution.py:9
  840.7 5.4 reduce_sum.152
  846.1 144.0 %all-gather.19.cloned.1.call-done = f32[4,4096,128]{2,1,0:T(8,128)} async-done(((f32[1,4096,128]{2,1,0:T(8,128)}), f32[4,4096,128]{2,1,0:T(8,128)}) %all-gather.19.cloned.1.call-update) | async-done | bytes 8388624 | tf_op jit(solution)/shard_map/all_gather | solution.py:9
  990.2 5.4 reduce_sum.153
  995.5 6.5 fusion.48
  1002.0 46.7 %all-reduce.13.cloned.1.call-done = (f32[256,1024]{1,0:T(8,128)}, f32[128,128]{1,0:T(8,128)}) async-done(((f32[256,1024]{1,0:T(8,128)}, f32[128,128]{1,0:T(8,128)}), (f32[256,1024]{1,0:T(8,128)}, f32[128,128]{1,0:T(8,128)})) %all-reduce.13.cloned.1.call-update) | async-done | bytes 1114128 | tf_op jit(solution)/shard_map/psum | solution.py:42
  1048.7 1.2 fusion.47
  1050.1 1.6 fusion.30
  1051.8 1.6 fusion.20
  1053.4 0.6 convolution_add_fusion.2
  1054.0 19.3 %convolution_subtract_fusion.2 = f32[4096,1024]{1,0:T(8,128)} fusion(f32[4096,1024]{1,0:T(8,128)} %convolution_subtract_fusion.3, f32[4096,128]{1,0:T(8,128)S(1)} %copy-done.1, f32[4096,128]{1,0:T(8,128)S(1)} %reduce_sum.148, f32[128,1024]{1,0:T(8,128)S(1)} %fusion.30, f32[128,1024]{1,0:T(8,128)S(1)} %convolution_add_fusion.2), kind=kOutput, calls=%fused_computation.2 | convolution fusion | flops 12890406912 | bytes 38797312 | tf_op jit(solution)/shard_map/dot_general | solution.py:23
  1073.3 30.0 %fusion.1 = f32[256,1024]{1,0:T(8,128)} fusion(f32[4096,1024]{1,0:T(8,128)} %convolution_subtract_fusion.2, f32[4096,128]{1,0:T(8,128)S(1)} %copy-done.8, f32[4096,128]{1,0:T(8,128)S(1)} %copy-done.6), kind=kOutput, calls=%fused_computation.9 | convolution fusion | flops 12885950464 | bytes 22020096 | tf_op jit(solution)/shard_map/dot_general | solution.py:13
  1103.4 21.9 %all_gather.74 = f32[4,128,128]{2,1,0:T(8,128)S(1)} all-gather(f32[1,128,128]{2,1,0:T(8,128)S(1)} %get-tuple-element.23), channel_id=1, replica_groups=mesh['row'=8,'col'=4] {'col'}, dimensions={0}, use_global_device_ids=true | all-gather | bytes 327680 | tf_op jit(solution)/shard_map/all_gather | solution.py:9
  1125.3 19.0 %all_gather.75 = f32[4,128,128]{2,1,0:T(8,128)S(1)} all-gather(f32[1,128,128]{2,1,0:T(8,128)S(1)} %get-tuple-element.25), channel_id=1, replica_groups=mesh['row'=8,'col'=4] {'col'}, dimensions={0}, use_global_device_ids=true | all-gather | bytes 327680 | tf_op jit(solution)/shard_map/all_gather | solution.py:9
  1144.3 63.2 %all-gather.21.cloned.1.call-done = f32[4,4096,128]{2,1,0:T(8,128)} async-done(((f32[1,4096,128]{2,1,0:T(8,128)}), f32[4,4096,128]{2,1,0:T(8,128)}) %all-gather.21.cloned.1.call-update) | async-done | bytes 8388624 | tf_op jit(solution)/shard_map/all_gather | solution.py:9
  1207.5 4.1 reduce_sum.156
  1211.6 145.2 %all-gather.23.cloned.1.call-done = f32[4,4096,128]{2,1,0:T(8,128)} async-done(((f32[1,4096,128]{2,1,0:T(8,128)}), f32[4,4096,128]{2,1,0:T(8,128)}) %all-gather.23.cloned.1.call-update) | async-done | bytes 8388624 | tf_op jit(solution)/shard_map/all_gather | solution.py:9
  1356.8 5.4 reduce_sum.157
  1362.2 5.7 fusion.50
  1367.9 47.5 %all-reduce.11.cloned.1.call-done = (f32[256,1024]{1,0:T(8,128)}, f32[128,128]{1,0:T(8,128)}) async-done(((f32[256,1024]{1,0:T(8,128)}, f32[128,128]{1,0:T(8,128)}), (f32[256,1024]{1,0:T(8,128)}, f32[128,128]{1,0:T(8,128)})) %all-reduce.11.cloned.1.call-update) | async-done | bytes 1114128 | tf_op jit(solution)/shard_map/psum | solution.py:42
  1415.4 1.2 fusion.49
  1416.5 1.7 fusion.18
  1418.3 1.6 fusion.27
  1420.1 1.6 convolution_add_fusion.1
  1421.8 18.8 %convolution_subtract_fusion.1 = f32[4096,1024]{1,0:T(8,128)} fusion(f32[4096,1024]{1,0:T(8,128)} %convolution_subtract_fusion.2, f32[4096,128]{1,0:T(8,128)S(1)} %copy-done.9, f32[4096,128]{1,0:T(8,128)S(1)} %copy-done.7, f32[128,1024]{1,0:T(8,128)S(1)} %fusion.27, f32[128,1024]{1,0:T(8,128)S(1)} %convolution_add_fusion.1), kind=kOutput, calls=%fused_computation.1 | convolution fusion | flops 12890406912 | bytes 38797312 | tf_op jit(solution)/shard_map/dot_general | solution.py:23
  1440.5 30.0 %fusion = f32[256,1024]{1,0:T(8,128)} fusion(f32[4096,1024]{1,0:T(8,128)} %convolution_subtract_fusion.1, f32[4096,128]{1,0:T(8,128)S(1)} %copy-done.10, f32[4096,128]{1,0:T(8,128)S(1)} %reduce_sum.156), kind=kOutput, calls=%fused_computation.8 | convolution fusion | flops 12885950464 | bytes 22020096 | tf_op jit(solution)/shard_map/dot_general | solution.py:13
  1470.6 14.0 all_gather.78
  1484.6 14.2 all_gather.79
  1498.8 28.3 %all-reduce.9.cloned.1.call-done = (f32[256,1024]{1,0:T(8,128)}, f32[128,128]{1,0:T(8,128)}) async-done(((f32[256,1024]{1,0:T(8,128)}, f32[128,128]{1,0:T(8,128)}), (f32[256,1024]{1,0:T(8,128)}, f32[128,128]{1,0:T(8,128)})) %all-reduce.9.cloned.1.call-update) | async-done | bytes 1114128 | tf_op jit(solution)/shard_map/psum | solution.py:42
  1527.1 1.2 fusion.51
  1528.3 1.6 fusion.16
  1529.9 1.6 fusion.24
  1531.8 0.6 convolution_add_fusion
  1532.4 18.5 %convolution_subtract_fusion = f32[4096,1024]{1,0:T(8,128)} fusion(f32[4096,1024]{1,0:T(8,128)} %convolution_subtract_fusion.1, f32[4096,128]{1,0:T(8,128)S(1)} %copy-done.11, f32[4096,128]{1,0:T(8,128)S(1)} %reduce_sum.156, f32[128,1024]{1,0:T(8,128)S(1)} %fusion.24, f32[128,1024]{1,0:T(8,128)S(1)} %convolution_add_fusion), kind=kOutput, calls=%fused_computation | convolution fusion | flops 12890406912 | bytes 38797312 | tf_op jit(solution)/shard_map/dot_general | solution.py:23
  (60 shorter events, 2.0 us)
Async XLA Ops:
  6.5 160.8 %all-gather.11.cloned.1.call-start = ((), (), s32[]{:S(2)}) async-start(), calls=%async_computation.1 | async-start | bytes 10485760 | tf_op jit(solution)/shard_map/all_gather | solution.py:9
  14.8 301.9 %all-gather.9.cloned.1.call-start = ((), (), s32[]{:S(2)}) async-start(), calls=%async_computation | async-start | bytes 10485760 | tf_op jit(solution)/shard_map/all_gather | solution.py:9
  15.6 458.9 %all-gather.13.cloned.1.call-start = ((), (), s32[]{:S(2)}) async-start(), calls=%async_computation.2 | async-start | bytes 10485760 | tf_op jit(solution)/shard_map/all_gather | solution.py:9
  16.3 607.4 %all-gather.15.cloned.1.call-start = ((), (), s32[]{:S(2)}) async-start(), calls=%async_computation.3 | async-start | bytes 10485760 | tf_op jit(solution)/shard_map/all_gather | solution.py:9
  16.9 665.2 %all-reduce.15.cloned.1.call-start = ((), (), s32[]{:S(2)}) async-start(), calls=%async_computation.11 | async-start | bytes 2228224 | tf_op jit(solution)/shard_map/psum | solution.py:42
  171.4 156.8 %copy-start.2 = (f32[4096,128]{1,0:T(8,128)}, f32[4096,128]{1,0:T(8,128)S(1)}, u32[]{:S(2)}) copy-start(f32[4096,128]{1,0:T(8,128)S(1)} %reduce_sum.145) | copy-start | bytes 6291460
  322.1 6.1 copy-start.4
  358.5 482.2 %all-gather.17.cloned.1.call-start = ((), (), s32[]{:S(2)}) async-start(), calls=%async_computation.4 | async-start | bytes 10485760 | tf_op jit(solution)/shard_map/all_gather | solution.py:9
  358.6 1.8 copy-start.14
  359.1 631.0 %all-gather.19.cloned.1.call-start = ((), (), s32[]{:S(2)}) async-start(), calls=%async_computation.5 | async-start | bytes 10485760 | tf_op jit(solution)/shard_map/all_gather | solution.py:9
  359.9 688.8 %all-reduce.13.cloned.1.call-start = ((), (), s32[]{:S(2)}) async-start(), calls=%async_computation.10 | async-start | bytes 2228224 | tf_op jit(solution)/shard_map/psum | solution.py:42
  682.1 6.3 copy-start.3
  682.1 6.3 copy-start.5
  688.4 19.5 %copy-start = (f32[4096,128]{1,0:T(8,128)S(1)}, f32[4096,128]{1,0:T(8,128)}, u32[]{:S(2)}) copy-start(f32[4096,128]{1,0:T(8,128)} %reduce_sum.149) | copy-start | bytes 6291460
  737.9 469.6 %all-gather.21.cloned.1.call-start = ((), (), s32[]{:S(2)}) async-start(), calls=%async_computation.6 | async-start | bytes 10485760 | tf_op jit(solution)/shard_map/all_gather | solution.py:9
  738.6 618.1 %all-gather.23.cloned.1.call-start = ((), (), s32[]{:S(2)}) async-start(), calls=%async_computation.7 | async-start | bytes 10485760 | tf_op jit(solution)/shard_map/all_gather | solution.py:9
  739.2 676.1 %all-reduce.11.cloned.1.call-start = ((), (), s32[]{:S(2)}) async-start(), calls=%async_computation.9 | async-start | bytes 2228224 | tf_op jit(solution)/shard_map/psum | solution.py:42
  1048.7 4.7 copy-start.12
  1048.7 5.3 copy-start.1
  1054.0 19.3 %copy-start.6 = (f32[4096,128]{1,0:T(8,128)S(1)}, f32[4096,128]{1,0:T(8,128)}, u32[]{:S(2)}) copy-start(f32[4096,128]{1,0:T(8,128)} %reduce_sum.152) | copy-start | bytes 6291460
  1054.0 19.3 %copy-start.8 = (f32[4096,128]{1,0:T(8,128)S(1)}, f32[4096,128]{1,0:T(8,128)}, u32[]{:S(2)}) copy-start(f32[4096,128]{1,0:T(8,128)} %reduce_sum.153) | copy-start | bytes 6291460
  1103.3 423.8 %all-reduce.9.cloned.1.call-start = ((), (), s32[]{:S(2)}) async-start(), calls=%async_computation.8 | async-start | bytes 2228224 | tf_op jit(solution)/shard_map/psum | solution.py:42
  1415.3 6.4 copy-start.7
  1415.4 6.4 copy-start.9
  1421.7 18.8 %copy-start.10 = (f32[4096,128]{1,0:T(8,128)S(1)}, f32[4096,128]{1,0:T(8,128)}, u32[]{:S(2)}) copy-start(f32[4096,128]{1,0:T(8,128)} %reduce_sum.157) | copy-start | bytes 6291460
  1527.1 4.7 copy-start.13
  1527.1 5.3 copy-start.11
Sparse Core Ops, SparseCore 0:
  14.9 152.3 all-gather.10
  168.9 147.7 all-gather.8
  318.3 156.1 all-gather.12
  475.8 147.8 all-gather.14
  626.8 55.2 all-reduce.14
  683.5 157.1 all-gather.16
  842.3 147.8 all-gather.18
  993.4 55.2 all-reduce.12
  1050.3 157.1 all-gather.20
  1208.9 147.8 all-gather.22
  1360.0 55.2 all-reduce.10
  1470.7 56.3 all-reduce.8
